TPU v7x, 32 devices: a whole 2x2x4 slice. The times are simulated.
32 devices in a mesh: grp: 4 (over x, core), tile: 8 (over z, y).
Axes of the slice: x: 2, y: 2, z: 4, core: 2. Of those that a mesh axis runs over, the one named last changes fastest.
Arguments:
- amplitudes: bfloat16 [40, 4, 245760], P(None, None, ('grp', 'tile')), may hold values from -6 to 6
- w_vvvo: bfloat16 [1024, 245760], P(None, ('grp', 'tile')), may hold values from -0.0234375 to 0.0234375
- pair_mask: int32 [1024], P(('grp', 'tile')), may hold values from 0 to 1, as said below
- owner_map: int32 [8], replicated, may hold values from 0 to 7, each once
Outputs:
- sigma_one: float32 [40, 4, 1024], P('tile', None, 'grp')
Inputs may be any that keep to these rules, and one draw needn't show every extreme that they name: `pair_mask`: in each aligned block of 32 pairs at most 24 are 1 and at least one is; some block has exactly 24 and some block exactly one. `owner_map`: a permutation of the row blocks.
All inputs are finite; a program needn't handle non-finite values.
Results may differ from a plain program's by a relative error of at most 0.0003.
Values sent between devices are 32-bit elements; how exact they have to be, the bound alone decides.
A program may use at most 128 MiB of HBM per device.

v0:
```python
import functools

import jax
import jax.numpy as jnp
from jax import lax
from jax.experimental import pallas as pl
from jax.experimental.pallas import tpu as pltpu
from jax.sharding import PartitionSpec as P

MESH = pl.DeviceIdType.MESH
LANES = 128


def chunk_width(total, limit):
    width = limit // LANES * LANES
    while total % width:
        width -= LANES
    return width


def nt_dot(left, right):
    return lax.dot_general(
        left, right, (((1,), (1,)), ((), ())), preferred_element_type=jnp.float32
    )


def mask_row(mask_ref, start, width, occ_width):
    tiles = []
    for tile_start in range(start, start + width, LANES):
        lane = lax.broadcasted_iota(jnp.int32, (8, LANES), 1) + tile_start
        first = tile_start // occ_width
        last = (tile_start + LANES - 1) // occ_width
        row = jnp.full((8, LANES), mask_ref[first], jnp.int32)
        for pair in range(first + 1, last + 1):
            row = jnp.where(lane >= pair * occ_width, mask_ref[pair], row)
        tiles.append(row)
    return jnp.concatenate(tiles, axis=1).astype(jnp.float32)


def kernel(
    planes, tiles, owner_ref, mask_ref, amp_hbm, w_hbm, out_ref,
    amp_raw, amp, keep_row, acc, w_vmem, core_src, core_dst, send_buf, recv_buf,
    amp_sem, w_sem, core_send, core_recv, send_sem, recv_sem,
):
    my_grp = lax.axis_index("grp")
    my_tile = lax.axis_index("tile")
    plane, core = my_grp // 2, my_grp % 2
    occ_total, roots, cols = amp_raw.shape
    occ_rows = occ_total // tiles
    rows = occ_rows * roots
    virt_rows = w_hbm.shape[0] // (2 * planes)
    lane_blocks = virt_rows // LANES
    occ_width = cols // mask_ref.shape[0]
    chunk = chunk_width(cols, 1280)

    def block_of(step):
        there = (plane + planes - 1 - step // 2) % planes
        own = step % 2
        return there * 2 + own * core + (1 - own) * (1 - core)

    def w_copy(step):
        start = pl.multiple_of(block_of(step) * virt_rows, virt_rows)
        return pltpu.make_async_copy(
            w_hbm.at[pl.ds(start, virt_rows)], w_vmem.at[step], w_sem.at[step]
        )

    amp_copy = pltpu.make_async_copy(amp_hbm, amp_raw, amp_sem)
    amp_copy.start()
    for step in range(2 * planes):
        w_copy(step).start()

    barrier = pltpu.get_barrier_semaphore()
    greeted = 0
    pl.semaphore_signal(
        barrier, inc=1, device_id={"grp": my_grp + 1 - 2 * core, "tile": my_tile},
        device_id_type=MESH,
    )
    greeted += 1
    for hop in range(planes):
        for shift in range(tiles):
            if hop or shift:
                pl.semaphore_signal(
                    barrier,
                    inc=1,
                    device_id={
                        "grp": (plane + hop) % planes * 2 + core,
                        "tile": (my_tile + shift) % tiles,
                    },
                    device_id_type=MESH,
                )
                greeted += 1

    for start in range(0, cols, chunk):
        keep_row[:, start : start + chunk] = mask_row(mask_ref, start, chunk, occ_width)

    amp_copy.wait()

    @pl.loop(0, cols // chunk)
    def _(part):
        columns = pl.ds(pl.multiple_of(part * chunk, chunk), chunk)
        keep = keep_row[0:1, columns].astype(jnp.bfloat16)
        for q in range(tiles):
            piece = amp_raw[pl.ds(owner_ref[q] * occ_rows, occ_rows), :, columns]
            amp[q * rows : (q + 1) * rows, columns] = piece.reshape(rows, chunk) * keep

    def core_copy(index):
        return pltpu.make_async_remote_copy(
            src_ref=core_src.at[index],
            dst_ref=core_dst.at[index],
            send_sem=core_send.at[index],
            recv_sem=core_recv.at[index],
            device_id={"grp": my_grp + 1 - 2 * core, "tile": my_tile},
            device_id_type=MESH,
        )

    def piece_copy(hop, shift):
        target = (my_tile + shift) % tiles
        return pltpu.make_async_remote_copy(
            src_ref=send_buf.at[hop, target],
            dst_ref=recv_buf.at[hop, shift],
            send_sem=send_sem.at[hop, shift],
            recv_sem=recv_sem.at[hop, shift],
            device_id={"grp": (plane + hop) % planes * 2 + core, "tile": target},
            device_id_type=MESH,
        )

    def each_piece():
        for q in range(tiles):
            for lb in range(lane_blocks):
                yield q, slice(lb * rows, (lb + 1) * rows), acc[
                    q * rows : (q + 1) * rows, lb * LANES : (lb + 1) * LANES
                ]

    @pl.loop(0, 2 * planes)
    def _(step):
        index = step // 2
        hop = planes - 1 - index
        w_copy(step).wait()
        acc[...] = nt_dot(amp[...], w_vmem[step])

        @pl.when(step == 0)
        def _():
            pl.semaphore_wait(barrier, greeted)

        @pl.when(step % 2 == 0)
        def _():
            for q, where, value in each_piece():
                core_src[index, q, where] = value
            core_copy(index).start()

        @pl.when(step % 2 == 1)
        def _():
            core_copy(index).wait_recv()
            for q, where, value in each_piece():
                send_buf[hop, q, where] = value + core_dst[index, q, where]
            for shift in reversed(range(1, tiles)):
                piece_copy(hop, shift).start()

            @pl.when(hop > 0)
            def _():
                piece_copy(hop, 0).start()

    total = send_buf[0, my_tile]
    sent = [
        (hop, shift)
        for hop in reversed(range(planes))
        for shift in range(tiles)
        if hop or shift
    ]
    for hop, shift in sent:
        piece_copy(hop, shift).wait_recv()
        total = total + recv_buf[hop, shift]
    for lb in range(lane_blocks):
        for i in range(occ_rows):
            at = lb * rows + i * roots
            out_ref[i, :, lb * LANES : (lb + 1) * LANES] = total[at : at + roots]
    for index in range(planes):
        core_copy(index).wait_send()
    for hop, shift in sent:
        piece_copy(hop, shift).wait_send()


def shards(amplitudes, w_vvvo, pair_mask, owner_map):
    occ_total, roots, cols = amplitudes.shape
    virt_total = w_vvvo.shape[0]
    grps, tiles = lax.axis_size("grp"), lax.axis_size("tile")
    planes = grps // 2
    occ_rows = occ_total // tiles
    virt_rows = virt_total // grps
    piece = (virt_rows // LANES * occ_rows * roots, LANES)
    return pl.pallas_call(
        functools.partial(kernel, planes, tiles),
        out_shape=jax.ShapeDtypeStruct((occ_rows, roots, virt_rows), jnp.float32),
        in_specs=[
            pl.BlockSpec(memory_space=pltpu.SMEM),
            pl.BlockSpec(memory_space=pltpu.SMEM),
            pl.BlockSpec(memory_space=pl.ANY),
            pl.BlockSpec(memory_space=pl.ANY),
        ],
        out_specs=pl.BlockSpec(memory_space=pltpu.VMEM),
        scratch_shapes=[
            pltpu.VMEM((occ_total, roots, cols), jnp.bfloat16),
            pltpu.VMEM((occ_total * roots, cols), jnp.bfloat16),
            pltpu.VMEM((8, cols), jnp.float32),
            pltpu.VMEM((occ_total * roots, virt_rows), jnp.float32),
            pltpu.VMEM((grps, virt_rows, cols), jnp.bfloat16),
            pltpu.VMEM((planes, tiles) + piece, jnp.float32),
            pltpu.VMEM((planes, tiles) + piece, jnp.float32),
            pltpu.VMEM((planes, tiles) + piece, jnp.float32),
            pltpu.VMEM((planes, tiles) + piece, jnp.float32),
            pltpu.SemaphoreType.DMA,
            pltpu.SemaphoreType.DMA((grps,)),
            pltpu.SemaphoreType.DMA((planes,)),
            pltpu.SemaphoreType.DMA((planes,)),
            pltpu.SemaphoreType.DMA((planes, tiles)),
            pltpu.SemaphoreType.DMA((planes, tiles)),
        ],
        compiler_params=pltpu.CompilerParams(
            collective_id=0, has_side_effects=True, vmem_limit_bytes=60 * 1024 * 1024
        ),
        name="sigma",
    )(owner_map, pair_mask, amplitudes, w_vvvo)


def solution(mesh):
    return jax.shard_map(
        shards,
        mesh=mesh,
        in_specs=(
            P(None, None, ("grp", "tile")),
            P(None, ("grp", "tile")),
            P(("grp", "tile")),
            P(),
        ),
        out_specs=P("tile", None, "grp"),
        check_vma=False,
    )
```

profile of v0, /device:TPU:0, one launch (start us, length us, event | category | flops | bytes accessed | tf_op | source)
XLA Modules:
  0.0 21.8 jit_solution(3251558500585378406)
XLA Ops:
  0.0 20.4 %sigma.1 = f32[5,4,256]{2,1,0:T(4,128)} custom-call(s32[8]{0:T(128)} %owner_ref.1, s32[32]{0:T(128)} %mask_ref.1, bf16[40,4,7680]{2,1,0:T(4,128)(2,1)} %amp_hbm.1, bf16[1024,7680]{1,0:T(8,128)(2,1)} %w_hbm.1), custom_call_target="tpu_custom_call" | custom-call | tf_op jit(solution)/shard_map/sigma/pallas_call | solution.py:191
  20.4 1.3 %copy.6 = f32[5,4,256]{2,1,0:T(4,128)} copy(f32[5,4,256]{2,1,0:T(4,128)} %sigma.1) | data formatting | bytes 40960
where the time goes:
time: 21.9 us; the launch traced here: 21.8 us
  Pallas kernels  20.4 us (93%)
  local copies, waits for them, and re-layouts  1.34 us (6%)
    pallas_call x1, Pallas kernels, shards(): pl.pallas_call(functools.partial(kernel, planes, tiles), out_shape=jax.Sh...  20.4 us
    unnamed x1, local copies, waits for them, and re-layouts  1.34 us

commit v1 on v0

--- a/solution.py
+++ b/solution.py
@@ -113,16 +113,17 @@
             device_id_type=MESH,
         )
 
-    def piece_copy(hop, shift):
-        target = (my_tile + shift) % tiles
+    def piece_copy(hop, target, source):
         return pltpu.make_async_remote_copy(
             src_ref=send_buf.at[hop, target],
-            dst_ref=recv_buf.at[hop, shift],
-            send_sem=send_sem.at[hop, shift],
-            recv_sem=recv_sem.at[hop, shift],
+            dst_ref=recv_buf.at[hop, source],
+            send_sem=send_sem.at[hop, target],
+            recv_sem=recv_sem.at[hop, source],
             device_id={"grp": (plane + hop) % planes * 2 + core, "tile": target},
             device_id_type=MESH,
         )
+
+    others = [index + (index >= my_tile).astype(jnp.int32) for index in map(jnp.int32, range(tiles - 1))]
 
     def each_piece():
         for q in range(tiles):
@@ -153,31 +154,34 @@
             core_copy(index).wait_recv()
             for q, where, value in each_piece():
                 send_buf[hop, q, where] = value + core_dst[index, q, where]
-            for shift in reversed(range(1, tiles)):
-                piece_copy(hop, shift).start()
 
             @pl.when(hop > 0)
             def _():
-                piece_copy(hop, 0).start()
+                for target in range(tiles):
+                    piece_copy(hop, target, my_tile).start()
+
+            @pl.when(hop == 0)
+            def _():
+                for other in others:
+                    piece_copy(hop, other, my_tile).start()
 
     total = send_buf[0, my_tile]
-    sent = [
-        (hop, shift)
+    pieces = [
+        (hop, tile)
         for hop in reversed(range(planes))
-        for shift in range(tiles)
-        if hop or shift
+        for tile in (range(tiles) if hop else others)
     ]
-    for hop, shift in sent:
-        piece_copy(hop, shift).wait_recv()
-        total = total + recv_buf[hop, shift]
+    for hop, tile in pieces:
+        piece_copy(hop, my_tile, tile).wait_recv()
+        total = total + recv_buf[hop, tile]
     for lb in range(lane_blocks):
         for i in range(occ_rows):
             at = lb * rows + i * roots
             out_ref[i, :, lb * LANES : (lb + 1) * LANES] = total[at : at + roots]
     for index in range(planes):
         core_copy(index).wait_send()
-    for hop, shift in sent:
-        piece_copy(hop, shift).wait_send()
+    for hop, tile in pieces:
+        piece_copy(hop, tile, my_tile).wait_send()
 
 
 def shards(amplitudes, w_vvvo, pair_mask, owner_map):
@@ -190,7 +194,7 @@
     piece = (virt_rows // LANES * occ_rows * roots, LANES)
     return pl.pallas_call(
         functools.partial(kernel, planes, tiles),
-        out_shape=jax.ShapeDtypeStruct((occ_rows, roots, virt_rows), jnp.float32),
+        out_shape=pltpu.VMEM((occ_rows, roots, virt_rows), jnp.float32),
         in_specs=[
             pl.BlockSpec(memory_space=pltpu.SMEM),
             pl.BlockSpec(memory_space=pltpu.SMEM),

time: 21.9 us -> 18.8 us (0.86)
  Pallas kernels: 20.4 us -> 18.1 us
  local copies, waits for them, and re-layouts: 1.34 us -> 0.61 us
    pallas_call x1, Pallas kernels: 20.4 us -> 18.1 us  [shards(): pl.pallas_call(functools.partial(kernel, planes, tiles), out_shape=pltpu....]
    unnamed x1, local copies, waits for them, and re-layouts: 1.34 us -> 0.61 us
where the time goes in v1:
time: 18.8 us; the launch traced here: 18.7 us
  Pallas kernels  18.1 us (96%)
  local copies, waits for them, and re-layouts  0.61 us (3%)
    pallas_call x1, Pallas kernels, shards(): pl.pallas_call(functools.partial(kernel, planes, tiles), out_shape=pltpu....  18.1 us
    unnamed x1, local copies, waits for them, and re-layouts  0.61 us

profile of v1, /device:TPU:0, one launch (start us, length us, event | category | flops | bytes accessed | tf_op | source)
XLA Modules:
  0.0 18.7 jit_solution(18001467468787987484)
XLA Ops:
  0.0 18.1 %sigma.1 = f32[5,4,256]{2,1,0:T(4,128)S(1)} custom-call(s32[8]{0:T(128)} %owner_ref.1, s32[32]{0:T(128)} %mask_ref.1, bf16[40,4,7680]{2,1,0:T(4,128)(2,1)} %amp_hbm.1, bf16[1024,7680]{1,0:T(8,128)(2,1)} %w_hbm.1), custom_call_target="tpu_custom_call" | custom-call | tf_op jit(solution)/shard_map/sigma/pallas_call | solution.py:195
  18.1 0.6 %copy.6 = f32[5,4,256]{2,1,0:T(4,128)} copy(f32[5,4,256]{2,1,0:T(4,128)S(1)} %sigma.1) | data formatting | bytes 40960

commit v2 on v1

--- a/solution.py
+++ b/solution.py
@@ -54,7 +54,7 @@
     chunk = chunk_width(cols, 1280)
 
     def block_of(step):
-        there = (plane + planes - 1 - step // 2) % planes
+        there = step // 2
         own = step % 2
         return there * 2 + own * core + (1 - own) * (1 - core)
 
@@ -135,7 +135,7 @@
     @pl.loop(0, 2 * planes)
     def _(step):
         index = step // 2
-        hop = planes - 1 - index
+        hop = (index + planes - plane) % planes
         w_copy(step).wait()
         acc[...] = nt_dot(amp[...], w_vmem[step])
 

time: 18.8 us -> 17.8 us (0.947)
  the two profiles are of different devices: /device:TPU:0 before, /device:TPU:10 now
where the time goes in v2:
time: 17.8 us; the launch traced here: 17.6 us
  Pallas kernels  17 us (96%)
  local copies, waits for them, and re-layouts  0.61 us (3%)
    pallas_call x1, Pallas kernels, shards(): pl.pallas_call(functools.partial(kernel, planes, tiles), out_shape=pltpu....  17 us
    unnamed x1, local copies, waits for them, and re-layouts  0.61 us

profile of v2, /device:TPU:10, one launch (start us, length us, event | category | flops | bytes accessed | tf_op | source)
XLA Modules:
  0.0 17.6 jit_solution(8186859074450003774)
XLA Ops:
  0.0 17.0 %sigma.1 = f32[5,4,256]{2,1,0:T(4,128)S(1)} custom-call(s32[8]{0:T(128)} %owner_ref.1, s32[32]{0:T(128)} %mask_ref.1, bf16[40,4,7680]{2,1,0:T(4,128)(2,1)} %amp_hbm.1, bf16[1024,7680]{1,0:T(8,128)(2,1)} %w_hbm.1), custom_call_target="tpu_custom_call" | custom-call | tf_op jit(solution)/shard_map/sigma/pallas_call | solution.py:195
  17.0 0.6 %copy.6 = f32[5,4,256]{2,1,0:T(4,128)} copy(f32[5,4,256]{2,1,0:T(4,128)S(1)} %sigma.1) | data formatting | bytes 40960

commit v3 on v2

--- a/solution.py
+++ b/solution.py
@@ -9,19 +9,7 @@
 
 MESH = pl.DeviceIdType.MESH
 LANES = 128
-
-
-def chunk_width(total, limit):
-    width = limit // LANES * LANES
-    while total % width:
-        width -= LANES
-    return width
-
-
-def nt_dot(left, right):
-    return lax.dot_general(
-        left, right, (((1,), (1,)), ((), ())), preferred_element_type=jnp.float32
-    )
+MXU = 256
 
 
 def mask_row(mask_ref, start, width, occ_width):
@@ -39,35 +27,55 @@
 
 def kernel(
     planes, tiles, owner_ref, mask_ref, amp_hbm, w_hbm, out_ref,
-    amp_raw, amp, keep_row, acc, w_vmem, core_src, core_dst, send_buf, recv_buf,
-    amp_sem, w_sem, core_send, core_recv, send_sem, recv_sem,
+    amp_raw, amp, keep_row, w_vmem, core_src, core_dst, own, send_buf, recv_buf,
+    amp_sem, first_sem, w_sem, core_send, core_recv, send_sem, recv_sem,
 ):
+    steps = 2 * planes
     my_grp = lax.axis_index("grp")
     my_tile = lax.axis_index("tile")
     plane, core = my_grp // 2, my_grp % 2
     occ_total, roots, cols = amp_raw.shape
     occ_rows = occ_total // tiles
     rows = occ_rows * roots
-    virt_rows = w_hbm.shape[0] // (2 * planes)
+    all_rows = occ_total * roots
+    virt_rows = w_hbm.shape[0] // steps
     lane_blocks = virt_rows // LANES
     occ_width = cols // mask_ref.shape[0]
-    chunk = chunk_width(cols, 1280)
+    filler = max(0, MXU - all_rows)
+    turns = cols // (2 * MXU)
+    cut = -(-turns // 2)
+    spans = ((0, cut), (cut, turns - cut))
 
     def block_of(step):
         there = step // 2
-        own = step % 2
-        return there * 2 + own * core + (1 - own) * (1 - core)
+        own_half = step % 2
+        return there * 2 + own_half * core + (1 - own_half) * (1 - core)
+
+    def rows_of(step):
+        return pl.ds(pl.multiple_of(block_of(step) * virt_rows, virt_rows), virt_rows)
 
     def w_copy(step):
-        start = pl.multiple_of(block_of(step) * virt_rows, virt_rows)
+        return pltpu.make_async_copy(w_hbm.at[rows_of(step)], w_vmem.at[step], w_sem.at[step])
+
+    def span_columns(part):
+        begin, count = spans[part]
+        return pl.ds(begin * 2 * MXU, count * 2 * MXU)
+
+    def first_copy(part):
+        where = span_columns(part)
         return pltpu.make_async_copy(
-            w_hbm.at[pl.ds(start, virt_rows)], w_vmem.at[step], w_sem.at[step]
+            w_hbm.at[rows_of(0), where], w_vmem.at[0, :, where], first_sem.at[part]
         )
 
-    amp_copy = pltpu.make_async_copy(amp_hbm, amp_raw, amp_sem)
-    amp_copy.start()
-    for step in range(2 * planes):
-        w_copy(step).start()
+    def amp_copy(part):
+        where = span_columns(part)
+        return pltpu.make_async_copy(
+            amp_hbm.at[:, :, where], amp_raw.at[:, :, where], amp_sem.at[part]
+        )
+
+    for part in range(2):
+        amp_copy(part).start()
+        first_copy(part).start()
 
     barrier = pltpu.get_barrier_semaphore()
     greeted = 0
@@ -90,18 +98,18 @@
                 )
                 greeted += 1
 
-    for start in range(0, cols, chunk):
-        keep_row[:, start : start + chunk] = mask_row(mask_ref, start, chunk, occ_width)
-
-    amp_copy.wait()
-
-    @pl.loop(0, cols // chunk)
-    def _(part):
-        columns = pl.ds(pl.multiple_of(part * chunk, chunk), chunk)
-        keep = keep_row[0:1, columns].astype(jnp.bfloat16)
-        for q in range(tiles):
-            piece = amp_raw[pl.ds(owner_ref[q] * occ_rows, occ_rows), :, columns]
-            amp[q * rows : (q + 1) * rows, columns] = piece.reshape(rows, chunk) * keep
+    width = 2 * MXU
+    for start in range(0, cols, width):
+        keep_row[:, start : start + width] = mask_row(mask_ref, start, width, occ_width)
+
+    def masked(part):
+        begin, count = spans[part]
+
+        @pl.loop(begin, begin + count)
+        def _(index):
+            where = pl.ds(pl.multiple_of(index * width, LANES), width)
+            keep = keep_row[0:1, where].astype(jnp.bfloat16)
+            amp[:, where] = amp_raw[:, :, where].reshape(all_rows, width) * keep
 
     def core_copy(index):
         return pltpu.make_async_remote_copy(
@@ -125,35 +133,61 @@
 
     others = [index + (index >= my_tile).astype(jnp.int32) for index in map(jnp.int32, range(tiles - 1))]
 
-    def each_piece():
-        for q in range(tiles):
+    def blocks(main0, main1, *pads):
+        mains = (main0, main1)
+
+        def unit_columns(turn, unit):
+            return pl.ds(pl.multiple_of(turn * 2 * MXU + unit * MXU, MXU), MXU)
+
+        def push(step, turn, slot):
+            for unit in range(2):
+                tile = w_vmem[step, :, unit_columns(turn, unit)]
+                pltpu.matmul_push_rhs(tile, slot, unit, transpose=True)
+
+        def multiply(turn, slot):
+            for unit in range(2):
+                left = amp[:, unit_columns(turn, unit)]
+                pltpu.matmul_acc_lhs(mains[unit], left, load_staged_rhs=slot)
+                if pads:
+                    pltpu.matmul_acc_lhs(pads[unit], jnp.zeros((filler, MXU), jnp.bfloat16))
+
+        def contract(step, begin, turns):
+            push(step, begin, 0)
+
+            @pl.loop(0, (turns - 1) // 2)
+            def _(trip):
+                turn = begin + trip * 2
+                push(step, turn + 1, 1)
+                multiply(turn, 0)
+                push(step, turn + 2, 0)
+                multiply(turn + 1, 1)
+
+            if turns % 2:
+                multiply(begin + turns - 1, 0)
+            else:
+                push(step, begin + turns - 1, 1)
+                multiply(begin + turns - 2, 0)
+                multiply(begin + turns - 1, 1)
+
+        def product():
+            return pltpu.matmul_pop(mains[0]) + pltpu.matmul_pop(mains[1])
+
+        def give(index):
+            value = product()
             for lb in range(lane_blocks):
-                yield q, slice(lb * rows, (lb + 1) * rows), acc[
-                    q * rows : (q + 1) * rows, lb * LANES : (lb + 1) * LANES
-                ]
-
-    @pl.loop(0, 2 * planes)
-    def _(step):
-        index = step // 2
-        hop = (index + planes - plane) % planes
-        w_copy(step).wait()
-        acc[...] = nt_dot(amp[...], w_vmem[step])
-
-        @pl.when(step == 0)
-        def _():
-            pl.semaphore_wait(barrier, greeted)
-
-        @pl.when(step % 2 == 0)
-        def _():
-            for q, where, value in each_piece():
-                core_src[index, q, where] = value
+                core_src[index, lb] = value[:, lb * LANES : (lb + 1) * LANES]
             core_copy(index).start()
 
-        @pl.when(step % 2 == 1)
-        def _():
+        def scatter(index):
+            hop = (index + planes - plane) % planes
+            value = product()
             core_copy(index).wait_recv()
-            for q, where, value in each_piece():
-                send_buf[hop, q, where] = value + core_dst[index, q, where]
+            for lb in range(lane_blocks):
+                own[lb] = value[:, lb * LANES : (lb + 1) * LANES] + core_dst[index, lb]
+            for q in range(tiles):
+                source = pl.ds(owner_ref[q] * rows, rows)
+                for lb in range(lane_blocks):
+                    send_buf[hop, q, lb * rows : (lb + 1) * rows] = own[lb, source]
 
             @pl.when(hop > 0)
             def _():
@@ -164,6 +198,43 @@
             def _():
                 for other in others:
                     piece_copy(hop, other, my_tile).start()
+
+        started = 1
+        for part, (begin, count) in enumerate(spans):
+            amp_copy(part).wait()
+            if started < steps:
+                w_copy(started).start()
+                started += 1
+            masked(part)
+            first_copy(part).wait()
+            contract(0, begin, count)
+        for step in range(started, steps):
+            w_copy(step).start()
+
+        pl.semaphore_wait(barrier, greeted)
+        give(0)
+
+        @pl.loop(1, steps)
+        def _(step):
+            w_copy(step).wait()
+            contract(step, 0, turns)
+
+            @pl.when(step % 2 == 0)
+            def _():
+                give(step // 2)
+
+            @pl.when(step % 2 == 1)
+            def _():
+                scatter(step // 2)
+
+        for pad in pads:
+            pltpu.matmul_pop(pad)
+
+    shapes = (all_rows,) + ((filler,) if filler else ())
+    pl.run_scoped(
+        blocks,
+        *(pltpu.ACC(unit)((size, MXU), jnp.float32) for size in shapes for unit in range(2)),
+    )
 
     total = send_buf[0, my_tile]
     pieces = [
@@ -191,6 +262,7 @@
     planes = grps // 2
     occ_rows = occ_total // tiles
     virt_rows = virt_total // grps
+    block = (virt_rows // LANES, occ_total * roots, LANES)
     piece = (virt_rows // LANES * occ_rows * roots, LANES)
     return pl.pallas_call(
         functools.partial(kernel, planes, tiles),
@@ -206,13 +278,14 @@
             pltpu.VMEM((occ_total, roots, cols), jnp.bfloat16),
             pltpu.VMEM((occ_total * roots, cols), jnp.bfloat16),
             pltpu.VMEM((8, cols), jnp.float32),
-            pltpu.VMEM((occ_total * roots, virt_rows), jnp.float32),
             pltpu.VMEM((grps, virt_rows, cols), jnp.bfloat16),
+            pltpu.VMEM((planes,) + block, jnp.float32),
+            pltpu.VMEM((planes,) + block, jnp.float32),
+            pltpu.VMEM(block, jnp.float32),
             pltpu.VMEM((planes, tiles) + piece, jnp.float32),
             pltpu.VMEM((planes, tiles) + piece, jnp.float32),
-            pltpu.VMEM((planes, tiles) + piece, jnp.float32),
-            pltpu.VMEM((planes, tiles) + piece, jnp.float32),
-            pltpu.SemaphoreType.DMA,
+            pltpu.SemaphoreType.DMA((2,)),
+            pltpu.SemaphoreType.DMA((2,)),
             pltpu.SemaphoreType.DMA((grps,)),
             pltpu.SemaphoreType.DMA((planes,)),
             pltpu.SemaphoreType.DMA((planes,)),

time: 17.8 us -> 17.5 us (0.983)
  Pallas kernels: 17 us -> 16.7 us
    pallas_call x1, Pallas kernels: 17 us -> 16.7 us  [shards(): pl.pallas_call(functools.partial(kernel, planes, tiles), out_shape=pltpu....]
where the time goes in v3:
time: 17.5 us; the launch traced here: 17.3 us
  Pallas kernels  16.7 us (95%)
  local copies, waits for them, and re-layouts  0.61 us (3%)
    pallas_call x1, Pallas kernels, shards(): pl.pallas_call(functools.partial(kernel, planes, tiles), out_shape=pltpu....  16.7 us
    unnamed x1, local copies, waits for them, and re-layouts  0.61 us

profile of v3, /device:TPU:10, one launch (start us, length us, event | category | flops | bytes accessed | tf_op | source)
XLA Modules:
  0.0 17.3 jit_solution(16372772030060919675)
XLA Ops:
  0.0 16.7 %sigma.1 = f32[5,4,256]{2,1,0:T(4,128)S(1)} custom-call(s32[8]{0:T(128)} %owner_ref.1, s32[32]{0:T(128)} %mask_ref.1, bf16[40,4,7680]{2,1,0:T(4,128)(2,1)} %amp_hbm.1, bf16[1024,7680]{1,0:T(8,128)(2,1)} %w_hbm.1), custom_call_target="tpu_custom_call" | custom-call | tf_op jit(solution)/shard_map/sigma/pallas_call | solution.py:267
  16.7 0.6 %copy.6 = f32[5,4,256]{2,1,0:T(4,128)} copy(f32[5,4,256]{2,1,0:T(4,128)S(1)} %sigma.1) | data formatting | bytes 40960

commit v4 on v3

--- a/solution.py
+++ b/solution.py
@@ -1,4 +1,5 @@
 import functools
+import math
 
 import jax
 import jax.numpy as jnp
@@ -12,15 +13,15 @@
 MXU = 256
 
 
-def mask_row(mask_ref, start, width, occ_width):
+def mask_row(mask_ref, base, width, occ_width):
     tiles = []
-    for tile_start in range(start, start + width, LANES):
+    for tile_start in range(0, width, LANES):
         lane = lax.broadcasted_iota(jnp.int32, (8, LANES), 1) + tile_start
         first = tile_start // occ_width
         last = (tile_start + LANES - 1) // occ_width
-        row = jnp.full((8, LANES), mask_ref[first], jnp.int32)
+        row = jnp.full((8, LANES), mask_ref[base + first], jnp.int32)
         for pair in range(first + 1, last + 1):
-            row = jnp.where(lane >= pair * occ_width, mask_ref[pair], row)
+            row = jnp.where(lane >= pair * occ_width, mask_ref[base + pair], row)
         tiles.append(row)
     return jnp.concatenate(tiles, axis=1).astype(jnp.float32)
 
@@ -76,6 +77,7 @@
     for part in range(2):
         amp_copy(part).start()
         first_copy(part).start()
+    w_copy(1).start()
 
     barrier = pltpu.get_barrier_semaphore()
     greeted = 0
@@ -84,23 +86,27 @@
         device_id_type=MESH,
     )
     greeted += 1
-    for hop in range(planes):
-        for shift in range(tiles):
-            if hop or shift:
+    @pl.loop(0, tiles)
+    def _(other):
+        for hop in range(planes):
+
+            @pl.when((hop > 0) | (other != my_tile))
+            def _(hop=hop):
                 pl.semaphore_signal(
                     barrier,
                     inc=1,
-                    device_id={
-                        "grp": (plane + hop) % planes * 2 + core,
-                        "tile": (my_tile + shift) % tiles,
-                    },
+                    device_id={"grp": (plane + hop) % planes * 2 + core, "tile": other},
                     device_id_type=MESH,
                 )
-                greeted += 1
-
+
+    greeted += planes * tiles - 1
     width = 2 * MXU
-    for start in range(0, cols, width):
-        keep_row[:, start : start + width] = mask_row(mask_ref, start, width, occ_width)
+    period = math.lcm(occ_width, LANES)
+
+    @pl.loop(0, cols // period)
+    def _(turn):
+        where = pl.ds(pl.multiple_of(turn * period, LANES), period)
+        keep_row[:, where] = mask_row(mask_ref, turn * (period // occ_width), period, occ_width)
 
     def masked(part):
         begin, count = spans[part]
@@ -184,22 +190,17 @@
             core_copy(index).wait_recv()
             for lb in range(lane_blocks):
                 own[lb] = value[:, lb * LANES : (lb + 1) * LANES] + core_dst[index, lb]
-            for q in range(tiles):
+            @pl.loop(0, tiles)
+            def _(q):
                 source = pl.ds(owner_ref[q] * rows, rows)
                 for lb in range(lane_blocks):
                     send_buf[hop, q, lb * rows : (lb + 1) * rows] = own[lb, source]
 
-            @pl.when(hop > 0)
-            def _():
-                for target in range(tiles):
-                    piece_copy(hop, target, my_tile).start()
-
-            @pl.when(hop == 0)
-            def _():
-                for other in others:
-                    piece_copy(hop, other, my_tile).start()
-
-        started = 1
+                @pl.when((hop > 0) | (q != my_tile))
+                def _():
+                    piece_copy(hop, q, my_tile).start()
+
+        started = 2
         for part, (begin, count) in enumerate(spans):
             amp_copy(part).wait()
             if started < steps:

time: 17.5 us -> 17.3 us (0.989)
  Pallas kernels: 16.7 us -> 16.5 us
    pallas_call x1, Pallas kernels: 16.7 us -> 16.5 us  [shards(): pl.pallas_call(functools.partial(kernel, planes, tiles), out_shape=pltpu....]
where the time goes in v4:
time: 17.3 us; the launch traced here: 17.1 us
  Pallas kernels  16.5 us (95%)
  local copies, waits for them, and re-layouts  0.61 us (4%)
    pallas_call x1, Pallas kernels, shards(): pl.pallas_call(functools.partial(kernel, planes, tiles), out_shape=pltpu....  16.5 us
    unnamed x1, local copies, waits for them, and re-layouts  0.61 us

profile of v4, /device:TPU:10, one launch (start us, length us, event | category | flops | bytes accessed | tf_op | source)
XLA Modules:
  0.0 17.1 jit_solution(7444214384525194667)
XLA Ops:
  0.0 16.5 %sigma.1 = f32[5,4,256]{2,1,0:T(4,128)S(1)} custom-call(s32[8]{0:T(128)} %owner_ref.1, s32[32]{0:T(128)} %mask_ref.1, bf16[40,4,7680]{2,1,0:T(4,128)(2,1)} %amp_hbm.1, bf16[1024,7680]{1,0:T(8,128)(2,1)} %w_hbm.1), custom_call_target="tpu_custom_call" | custom-call | tf_op jit(solution)/shard_map/sigma/pallas_call | solution.py:268
  16.5 0.6 %copy.6 = f32[5,4,256]{2,1,0:T(4,128)} copy(f32[5,4,256]{2,1,0:T(4,128)S(1)} %sigma.1) | data formatting | bytes 40960
